TPU v7x, 32 devices: a whole 2x2x4 slice. The times are simulated.
32 devices in a mesh: rows: 8 (over z, x), cols: 4 (over y, core).
Axes of the slice: x: 2, y: 2, z: 4, core: 2. Of those that a mesh axis runs over, the one named last changes fastest.
Arguments:
- lattice: int32 [256, 16384], P('rows', 'cols'), may hold values from -1 to 1, as said below
- draws: int32 [2, 256, 16384], P(None, 'rows', 'cols'), may hold values from -2147483648 to 2147483647, as said below
- thresholds: int32 [5], replicated, may hold values from 32 to 256
Outputs:
- final_lattice: int32 [256, 16384], P('rows', 'cols')
- row_magnetization: float32 [256], P('rows')
Inputs may be any that keep to these rules, and one draw needn't show every extreme that they name: `lattice`: every entry is -1 or 1. Each word holds four independent draws of 0 to 255: bits 8k to 8k+7 of draws[p] belong to sweep 4p + k.
All inputs are finite; a program needn't handle non-finite values.
Results may differ from a plain program's by a relative error of at most 0.0003.
Values sent between devices are 32-bit elements; how exact they have to be, the bound alone decides.
A program may use at most 64 MiB of HBM per device.

v0:
```python
import functools

import jax
import jax.numpy as jnp
from jax import lax
from jax.experimental import pallas as pl
from jax.experimental.pallas import tpu as pltpu
from jax.sharding import PartitionSpec as P

SWEEPS = 8
LEVELS = 5
PER_WORD = 4
BITS = 8
DEPTH = 8
LANES = 128
WORD = 32
MESH = pl.DeviceIdType.MESH

shr = lax.shift_right_logical


def transposed(words):
    words = list(words)
    mask = 0x0000FFFF
    j = 16
    while j:
        signed = mask - (1 << 32) if mask >> 31 else mask
        for k in range(WORD):
            if k & j:
                continue
            low, high = words[k], words[k + j]
            t = (shr(low, jnp.int32(j)) ^ high) & jnp.int32(signed)
            words[k + j] = high ^ t
            words[k] = low ^ (t << j)
        j >>= 1
        mask = (mask ^ (mask << j)) & 0xFFFFFFFF
    return words


def accept_masks(planes, bit_masks):
    below = []
    for level in range(LEVELS):
        t = bit_masks[level]
        z = planes[0] & t[0]
        for b in range(1, BITS):
            z = (z ^ (t[b - 1] ^ t[b])) & (planes[b] ^ ~t[b])
        below.append((z ^ t[BITS - 1]) | t[BITS])
    return below[0], below[0] ^ below[1], below[2], below[2] ^ below[3], below[0] ^ below[4]


def lane_neighbours(main, side, lane):
    rm, rs = pltpu.roll(main, 1, 1), pltpu.roll(side, 1, 1)
    sm, ss = pltpu.roll(main, LANES - 1, 1), pltpu.roll(side, LANES - 1, 1)
    first, last = lane == 0, lane == LANES - 1
    left_m = jnp.where(first, (rm << 1) | (rs & 1), rm)
    left_s = jnp.where(first, shr(rm, jnp.int32(30)) & 2, rs)
    right_m = jnp.where(last, shr(sm, jnp.int32(1)) | ((ss & 2) << 30), sm)
    right_s = jnp.where(last, sm & 1, ss)
    return (left_m, right_m), (left_s, right_s)


def updated(word, across, accept, colour_mask):
    rows = word.shape[0]
    a0, d1, a2, d3, d4 = accept
    x1, x2 = pltpu.roll(word, 1, 0) ^ word, pltpu.roll(word, rows - 1, 0) ^ word
    x3, x4 = across[0] ^ word, across[1] ^ word
    p, c1 = x1 ^ x2, ~(x1 | x2)
    q, c2 = x3 ^ x4, ~(x3 | x4)
    ones, twos, fours = p ^ q, (c1 ^ c2) | (p & q), c1 & c2
    low, high = a0 ^ (ones & d1), a2 ^ (ones & d3)
    take = low ^ (twos & (low ^ high)) ^ (fours & d4)
    return word ^ (take & colour_mask)


def sweep_kernel(shape, lat_ref, draws_ref, thr_ref, word_ref, mean_ref,
                 spins, draws, accept, state, out_edge, in_edge, count, peers,
                 local_sem, send_sem, recv_sem, edge_send, edge_recv, peer_send, peer_recv):
    n_rows, n_cols = shape
    rows, cols = lat_ref.shape
    tiles = cols // LANES
    packs = draws_ref.shape[0]
    ext = rows + 2 * DEPTH
    r, c = lax.axis_index("rows"), lax.axis_index("cols")
    up, down = lax.rem(r + n_rows - 1, n_rows), lax.rem(r + 1, n_rows)
    left, right = lax.rem(c + n_cols - 1, n_cols), lax.rem(c + 1, n_cols)

    local = [pltpu.make_async_copy(lat_ref, spins.at[pl.ds(DEPTH, rows), pl.ds(0, cols)], local_sem.at[0])]
    for pack in range(packs):
        local.append(pltpu.make_async_copy(
            draws_ref.at[pack], draws.at[pack, pl.ds(DEPTH, rows), pl.ds(0, cols)], local_sem.at[1 + pack]))
    for copy in local:
        copy.start()

    barrier = pltpu.get_barrier_semaphore()
    around = [(a, b) for a in (up, r, down) for b in (left, c, right)]
    del around[4]
    others = [lax.rem(c + k, n_cols) for k in range(1, n_cols)]
    for target in around + [(r, b) for b in others[1:-1]]:
        pl.semaphore_signal(barrier, inc=1, device_id=target, device_id_type=MESH)
    pl.semaphore_wait(barrier, len(around) + n_cols - 3)

    row_part = {-1: (0, DEPTH, DEPTH + rows), 0: (0, rows, DEPTH), 1: (rows - DEPTH, DEPTH, 0)}
    col_part = {-1: (0, LANES, cols + LANES), 0: (0, cols, 0), 1: (cols - LANES, LANES, cols)}
    row_id = {-1: up, 0: r, 1: down}
    col_id = {-1: left, 0: c, 1: right}
    sides = [(-1, 0), (1, 0), (0, -1), (0, 1), (-1, -1), (-1, 1), (1, -1), (1, 1)]
    first, later = [], []
    for stage in range(1 + packs):
        for index, (dr, dc) in enumerate(sides):
            r0, rn, rd = row_part[dr]
            c0, cn, cd = col_part[dc]
            src, dst = (lat_ref, spins) if stage == 0 else (draws_ref.at[stage - 1], draws.at[stage - 1])
            copy = pltpu.make_async_remote_copy(
                src_ref=src.at[pl.ds(r0, rn), pl.ds(c0, cn)],
                dst_ref=dst.at[pl.ds(rd, rn), pl.ds(cd, cn)],
                send_sem=send_sem.at[stage, index],
                recv_sem=recv_sem.at[stage, index],
                device_id=(row_id[dr], col_id[dc]),
                device_id_type=MESH,
            )
            copy.start()
            (first if stage <= 1 else later).append(copy)

    bit_masks = []
    for level in range(LEVELS):
        t = thr_ref[level]
        bit_masks.append([-((t >> b) & 1) for b in range(BITS + 1)])

    def tile_of(ref, row0, b):
        return ref[pl.ds(row0, 8), pl.ds(b * LANES, LANES)]

    def prepare(pack, group):
        row0 = pl.multiple_of(group * 8, 8)
        source = draws.at[pack]
        planes = transposed([tile_of(source, row0, b) for b in range(tiles)])
        for t in range(PER_WORD):
            masks = accept_masks(planes[BITS * t:BITS * (t + 1)], bit_masks)
            for k in range(LEVELS):
                accept[pack * PER_WORD + t, k, 0, pl.ds(row0, 8), :] = masks[k]

    def prepare_side(pack, group):
        row0 = pl.multiple_of(group * 8, 8)
        source = draws.at[pack]
        lo, hi = tile_of(source, row0, tiles), tile_of(source, row0, tiles + 1)
        even = (lo & 0x55555555) | ((hi & 0x55555555) << 1)
        odd = (shr(lo, jnp.int32(1)) & 0x55555555) | (hi & -0x55555556)
        planes = [shr((even, odd)[q & 1], jnp.int32(q & ~1)) for q in range(WORD)]
        for t in range(PER_WORD):
            masks = accept_masks(planes[BITS * t:BITS * (t + 1)], bit_masks)
            for k in range(LEVELS):
                accept[pack * PER_WORD + t, k, 1, pl.ds(row0, 8), :] = masks[k]

    def pack_group(group):
        row0 = pl.multiple_of(group * 8, 8)
        word = shr(tile_of(spins, row0, 0), jnp.int32(31))
        for b in range(1, tiles):
            word = word | (tile_of(spins, row0, b) & jnp.int32(-(1 << 31) if b == 31 else 1 << b))
        state[0, pl.ds(row0, 8), :] = word

    def pack_side(group):
        row0 = pl.multiple_of(group * 8, 8)
        state[1, pl.ds(row0, 8), :] = shr(tile_of(spins, row0, tiles), jnp.int32(31)) | (
            tile_of(spins, row0, tiles + 1) & 2)

    groups = rows // 8
    halo = DEPTH // 8

    for copy in local:
        copy.wait()

    @pl.loop(halo, halo + groups)
    def _(group):
        pack_group(group)

    @pl.loop(0, packs * groups)
    def _(step):
        prepare(step // groups, halo + step % groups)

    for copy in first:
        copy.wait()

    @pl.loop(halo, halo + groups)
    def _(group):
        pack_side(group)

    for group in (0, halo + groups):
        pack_group(group)
        pack_side(group)

    @pl.loop(0, 2)
    def _(side):
        prepare(0, side * (halo + groups))

    @pl.loop(0, groups + 2 * halo)
    def _(group):
        prepare_side(0, group)

    lane = lax.broadcasted_iota(jnp.int32, (ext, LANES), 1)
    base = r * rows + c * cols - DEPTH
    site = lax.broadcasted_iota(jnp.int32, (ext, LANES), 0) + lane + base
    odd_sites = -(site & 1)

    def sweep(sweep_no):
        main, side = state[0], state[1]
        for colour_mask in (~odd_sites, odd_sites):
            across_m, across_s = lane_neighbours(main, side, lane)
            main, side = (
                updated(main, across_m, [accept[sweep_no, k, 0] for k in range(LEVELS)], colour_mask),
                updated(side, across_s, [accept[sweep_no, k, 1] for k in range(LEVELS)], colour_mask),
            )
        state[0] = main
        state[1] = side

    half = DEPTH // 2

    @pl.loop(0, half)
    def _(t):
        sweep(t)

    copies = []
    for index, (row0, dev) in enumerate(((DEPTH, up), (rows, down))):
        main, side = state[0, pl.ds(row0, DEPTH), :], state[1, pl.ds(row0, DEPTH), :]
        for b in range(tiles):
            out_edge[index, :, pl.ds(b * LANES, LANES)] = shr(main, jnp.int32(b)) & 1
        for b in range(2):
            out_edge[index, :, pl.ds(cols + b * LANES, LANES)] = shr(side, jnp.int32(b)) & 1
        copy = pltpu.make_async_remote_copy(
            src_ref=out_edge.at[index],
            dst_ref=in_edge.at[index],
            send_sem=edge_send.at[index],
            recv_sem=edge_recv.at[index],
            device_id=(dev, c),
            device_id_type=MESH,
        )
        copy.start()
        copies.append(copy)

    for copy in later:
        copy.wait()

    @pl.loop(0, 2)
    def _(side):
        prepare(1, side * (halo + groups))

    @pl.loop(0, groups + 2 * halo)
    def _(group):
        prepare_side(1, group)

    for index, (row0, copy) in enumerate(((DEPTH + rows, copies[0]), (0, copies[1]))):
        copy.wait()
        word = in_edge[index, :, pl.ds(0, LANES)]
        for b in range(1, tiles):
            word = word | (in_edge[index, :, pl.ds(b * LANES, LANES)] << b)
        state[0, pl.ds(row0, DEPTH), :] = word
        state[1, pl.ds(row0, DEPTH), :] = in_edge[index, :, pl.ds(cols, LANES)] | (
            in_edge[index, :, pl.ds(cols + LANES, LANES)] << 1)

    @pl.loop(half, SWEEPS)
    def _(t):
        sweep(t)

    final = state[0, pl.ds(DEPTH, rows), :]
    word_ref[...] = final
    count[...] = lax.population_count(final)
    copies = []
    for k in range(1, n_cols):
        copy = pltpu.make_async_remote_copy(
            src_ref=count,
            dst_ref=peers.at[k - 1],
            send_sem=peer_send.at[k - 1],
            recv_sem=peer_recv.at[k - 1],
            device_id=(r, others[k - 1]),
            device_id_type=MESH,
        )
        copy.start()
        copies.append(copy)
    total = count[...]
    for k in range(1, n_cols):
        copies[k - 1].wait()
        total = total + peers[k - 1]
    downs = jnp.sum(total.astype(jnp.float32), axis=1, keepdims=True)
    width = n_cols * cols
    mean = (width - 2.0 * downs) / width
    at = lax.broadcasted_iota(jnp.int32, (rows, LANES), 0) == lax.broadcasted_iota(jnp.int32, (rows, LANES), 1)
    mean_ref[...] = jnp.sum(jnp.where(at, mean, 0.0), axis=0, keepdims=True)


def unpack_kernel(word_ref, row_ref, lattice_ref, mean_ref):
    word = word_ref[...]
    for b in range(lattice_ref.shape[1] // LANES):
        lattice_ref[:, b * LANES:(b + 1) * LANES] = 1 - ((shr(word, jnp.int32(b)) & 1) << 1)
    mean_ref[...] = row_ref[...]


def on_device(shape, lattice, draws, thresholds):
    rows, cols = lattice.shape
    packs = draws.shape[0]
    assert cols == WORD * LANES and rows <= LANES and rows % 8 == 0 and 2 * DEPTH == 2 * SWEEPS
    ext, wide = rows + 2 * DEPTH, cols + 2 * LANES
    n_cols = shape[1]
    vmem, hbm = pltpu.VMEM, pl.ANY
    word, mean = pl.pallas_call(
        functools.partial(sweep_kernel, shape),
        out_shape=(
            jax.ShapeDtypeStruct((rows, LANES), jnp.int32),
            jax.ShapeDtypeStruct((1, LANES), jnp.float32),
        ),
        in_specs=[
            pl.BlockSpec(memory_space=hbm),
            pl.BlockSpec(memory_space=hbm),
            pl.BlockSpec(memory_space=pltpu.SMEM),
        ],
        out_specs=(pl.BlockSpec(memory_space=vmem), pl.BlockSpec(memory_space=vmem)),
        scratch_shapes=[
            vmem((ext, wide), jnp.int32),
            vmem((packs, ext, wide), jnp.int32),
            vmem((SWEEPS, LEVELS, 2, ext, LANES), jnp.int32),
            vmem((2, ext, LANES), jnp.int32),
            vmem((2, DEPTH, wide), jnp.int32),
            vmem((2, DEPTH, wide), jnp.int32),
            vmem((rows, LANES), jnp.int32),
            vmem((n_cols - 1, rows, LANES), jnp.int32),
            pltpu.SemaphoreType.DMA((1 + packs,)),
            pltpu.SemaphoreType.DMA((1 + packs, 8)),
            pltpu.SemaphoreType.DMA((1 + packs, 8)),
            pltpu.SemaphoreType.DMA((2,)),
            pltpu.SemaphoreType.DMA((2,)),
            pltpu.SemaphoreType.DMA((n_cols - 1,)),
            pltpu.SemaphoreType.DMA((n_cols - 1,)),
        ],
        compiler_params=pltpu.CompilerParams(collective_id=0, has_side_effects=True),
        name="sweeps",
    )(lattice, draws, thresholds)
    final, means = pl.pallas_call(
        unpack_kernel,
        out_shape=(
            jax.ShapeDtypeStruct((rows, cols), jnp.int32),
            jax.ShapeDtypeStruct((1, LANES), jnp.float32),
        ),
        name="unpack",
    )(word, mean)
    return final, means[0, :rows]


def solution(mesh):
    shape = (mesh.shape["rows"], mesh.shape["cols"])
    in_specs = (P("rows", "cols"), P(None, "rows", "cols"), P())
    out_specs = (P("rows", "cols"), P("rows"))
    return jax.shard_map(
        functools.partial(on_device, shape), mesh=mesh, in_specs=in_specs, out_specs=out_specs, check_vma=False
    )
```

profile of v0, /device:TPU:0, one launch (start us, length us, event | category | flops | bytes accessed | tf_op | source)
XLA Modules:
  0.0 41.1 jit_solution(14346582237343340049)
XLA Ops:
  0.6 37.7 %sweeps.1 = (s32[32,128]{1,0:T(8,128)}, f32[1,128]{1,0:T(1,128)}) custom-call(s32[32,4096]{1,0:T(8,128)} %lat_ref.1, s32[2,32,4096]{2,1,0:T(8,128)} %draws_ref.1, s32[5]{0:T(128)} %thr_ref.1), custom_call_target="tpu_custom_call" | custom-call | tf_op jit(solution)/shard_map/sweeps/pallas_call | solution.py:302
  38.3 1.6 %unpack.1 = (s32[32,4096]{1,0:T(8,128)}, f32[1,128]{1,0:T(1,128)}) custom-call(s32[32,128]{1,0:T(8,128)} %get-tuple-element.6.word_ref, f32[1,128]{1,0:T(1,128)} %get-tuple-element.7.row_ref), custom_call_target="tpu_custom_call" | custom-call | tf_op jit(solution)/shard_map/unpack/pallas_call | solution.py:334
  39.9 0.0 copy-start
  39.9 0.7 %copy-done = f32[1,128]{1,0:T(1,128)S(1)} copy-done((f32[1,128]{1,0:T(1,128)S(1)}, f32[1,128]{1,0:T(1,128)}, u32[]{:S(2)}) %copy-start) | copy-done | bytes 536
  40.6 0.5 %slice_bitcast_fusion = f32[32]{0:T(128)} fusion(f32[1,128]{1,0:T(1,128)S(1)} %copy-done), kind=kLoop, calls=%fused_computation | loop fusion | bytes 256 | tf_op jit(solution)/shard_map/squeeze | solution.py:342
Async XLA Ops:
  39.9 0.7 %copy-start = (f32[1,128]{1,0:T(1,128)S(1)}, f32[1,128]{1,0:T(1,128)}, u32[]{:S(2)}) copy-start(f32[1,128]{1,0:T(1,128)} %get-tuple-element.9) | copy-start | bytes 1540
where the time goes:
time: 41.3 us; the launch traced here: 41.1 us
  Pallas kernels  39.3 us (95%)
  local copies, waits for them, and re-layouts  1.17 us (3%)
  between operations  0.64 us (2%)
    pallas_call x1, Pallas kernels, on_device(): pl.pallas_call(functools.partial(sweep_kernel, shape), out_shape=(jax.Sha...  37.7 us
    pallas_call x1, Pallas kernels, on_device(): pl.pallas_call(unpack_kernel, out_shape=(jax.ShapeDtypeStruct((rows, cols...  1.58 us

commit v1 on v0

--- a/solution.py
+++ b/solution.py
@@ -99,27 +99,39 @@
         pl.semaphore_signal(barrier, inc=1, device_id=target, device_id_type=MESH)
     pl.semaphore_wait(barrier, len(around) + n_cols - 3)
 
-    row_part = {-1: (0, DEPTH, DEPTH + rows), 0: (0, rows, DEPTH), 1: (rows - DEPTH, DEPTH, 0)}
+    def row_part(depth):
+        return {-1: (0, depth, DEPTH + rows), 0: (0, rows, DEPTH), 1: (rows - depth, depth, DEPTH - depth)}
+
     col_part = {-1: (0, LANES, cols + LANES), 0: (0, cols, 0), 1: (cols - LANES, LANES, cols)}
     row_id = {-1: up, 0: r, 1: down}
     col_id = {-1: left, 0: c, 1: right}
-    sides = [(-1, 0), (1, 0), (0, -1), (0, 1), (-1, -1), (-1, 1), (1, -1), (1, 1)]
-    first, later = [], []
+    sides = [(0, -1), (0, 1), (-1, -1), (-1, 1), (1, -1), (1, 1), (-1, 0), (1, 0)]
+    strips, first, later = [], [], []
+
+    def send(stage, index):
+        dr, dc = sides[index]
+        r0, rn, rd = row_part(DEPTH - min(stage, 1))[dr]
+        c0, cn, cd = col_part[dc]
+        src, dst = (lat_ref, spins) if stage == 0 else (draws_ref.at[stage - 1], draws.at[stage - 1])
+        copy = pltpu.make_async_remote_copy(
+            src_ref=src.at[pl.ds(r0, rn), pl.ds(c0, cn)],
+            dst_ref=dst.at[pl.ds(rd, rn), pl.ds(cd, cn)],
+            send_sem=send_sem.at[stage, index],
+            recv_sem=recv_sem.at[stage, index],
+            device_id=(row_id[dr], col_id[dc]),
+            device_id_type=MESH,
+        )
+        copy.start()
+        return copy
+
     for stage in range(1 + packs):
-        for index, (dr, dc) in enumerate(sides):
-            r0, rn, rd = row_part[dr]
-            c0, cn, cd = col_part[dc]
-            src, dst = (lat_ref, spins) if stage == 0 else (draws_ref.at[stage - 1], draws.at[stage - 1])
-            copy = pltpu.make_async_remote_copy(
-                src_ref=src.at[pl.ds(r0, rn), pl.ds(c0, cn)],
-                dst_ref=dst.at[pl.ds(rd, rn), pl.ds(cd, cn)],
-                send_sem=send_sem.at[stage, index],
-                recv_sem=recv_sem.at[stage, index],
-                device_id=(row_id[dr], col_id[dc]),
-                device_id_type=MESH,
-            )
-            copy.start()
-            (first if stage <= 1 else later).append(copy)
+        strips += [send(stage, index) for index in (0, 1)]
+    for stage in range(1 + packs):
+        copies = [send(stage, index) for index in range(2, len(sides))]
+        if stage <= 1:
+            first += copies
+        else:
+            later += copies
 
     bit_masks = []
     for level in range(LEVELS):
@@ -176,13 +188,20 @@
     def _(step):
         prepare(step // groups, halo + step % groups)
 
-    for copy in first:
+    for copy in strips:
         copy.wait()
 
     @pl.loop(halo, halo + groups)
     def _(group):
         pack_side(group)
 
+    @pl.loop(0, packs * groups)
+    def _(step):
+        prepare_side(step // groups, halo + step % groups)
+
+    for copy in first:
+        copy.wait()
+
     for group in (0, halo + groups):
         pack_group(group)
         pack_side(group)
@@ -190,10 +209,7 @@
     @pl.loop(0, 2)
     def _(side):
         prepare(0, side * (halo + groups))
-
-    @pl.loop(0, groups + 2 * halo)
-    def _(group):
-        prepare_side(0, group)
+        prepare_side(0, side * (halo + groups))
 
     lane = lax.broadcasted_iota(jnp.int32, (ext, LANES), 1)
     base = r * rows + c * cols - DEPTH
@@ -218,12 +234,19 @@
         sweep(t)
 
     copies = []
+    tile_id = lax.broadcasted_iota(jnp.int32, (WORD, LANES), 0)
+    sub, lane8 = (lax.broadcasted_iota(jnp.int32, (DEPTH, LANES), d) for d in (0, 1))
+    low_lanes = lane8 < LANES // 2
+    near, far = (0, DEPTH - 1), (DEPTH - 1, 0)
     for index, (row0, dev) in enumerate(((DEPTH, up), (rows, down))):
         main, side = state[0, pl.ds(row0, DEPTH), :], state[1, pl.ds(row0, DEPTH), :]
-        for b in range(tiles):
-            out_edge[index, :, pl.ds(b * LANES, LANES)] = shr(main, jnp.int32(b)) & 1
-        for b in range(2):
-            out_edge[index, :, pl.ds(cols + b * LANES, LANES)] = shr(side, jnp.int32(b)) & 1
+        odd = odd_sites[row0:row0 + DEPTH]
+        joint = (main & odd) | (pltpu.roll(main, 1 if index == 0 else DEPTH - 1, 0) & ~odd)
+        main = jnp.where(sub == near[index], joint, main)
+        for i in range(DEPTH - 1):
+            row = main[i + index:i + index + 1]
+            out_edge[index, pl.ds(i * WORD, WORD), :] = shr(jnp.broadcast_to(row, (WORD, LANES)), tile_id) & 1
+        out_edge[index, pl.ds((DEPTH - 1) * WORD, DEPTH), :] = jnp.where(low_lanes, shr(side, jnp.int32(1)), side) & 1
         copy = pltpu.make_async_remote_copy(
             src_ref=out_edge.at[index],
             dst_ref=in_edge.at[index],
@@ -241,19 +264,26 @@
     @pl.loop(0, 2)
     def _(side):
         prepare(1, side * (halo + groups))
-
-    @pl.loop(0, groups + 2 * halo)
-    def _(group):
-        prepare_side(1, group)
+        prepare_side(1, side * (halo + groups))
 
     for index, (row0, copy) in enumerate(((DEPTH + rows, copies[0]), (0, copies[1]))):
         copy.wait()
-        word = in_edge[index, :, pl.ds(0, LANES)]
-        for b in range(1, tiles):
-            word = word | (in_edge[index, :, pl.ds(b * LANES, LANES)] << b)
+        old = state[0, pl.ds(row0, DEPTH), :]
+        odd = odd_sites[row0:row0 + DEPTH]
+        word = old
+        for i in range(DEPTH - 1):
+            bits = in_edge[index, pl.ds(i * WORD, WORD), :] << tile_id
+            row = bits[0:8] | bits[8:16] | bits[16:24] | bits[24:32]
+            for shift in (4, 2, 1):
+                row = row | pltpu.roll(row, shift, 0)
+            at = i + index
+            if at == near[index]:
+                word = jnp.where(sub == far[index], row, word)
+                row = (old & ~odd) | (row & odd)
+            word = jnp.where(sub == at, row, word)
         state[0, pl.ds(row0, DEPTH), :] = word
-        state[1, pl.ds(row0, DEPTH), :] = in_edge[index, :, pl.ds(cols, LANES)] | (
-            in_edge[index, :, pl.ds(cols + LANES, LANES)] << 1)
+        bits = in_edge[index, pl.ds((DEPTH - 1) * WORD, DEPTH), :]
+        state[1, pl.ds(row0, DEPTH), :] = jnp.where(low_lanes, bits << 1, bits)
 
     @pl.loop(half, SWEEPS)
     def _(t):
@@ -289,7 +319,7 @@
     word = word_ref[...]
     for b in range(lattice_ref.shape[1] // LANES):
         lattice_ref[:, b * LANES:(b + 1) * LANES] = 1 - ((shr(word, jnp.int32(b)) & 1) << 1)
-    mean_ref[...] = row_ref[...]
+    mean_ref[...] = row_ref[0, :mean_ref.shape[0]]
 
 
 def on_device(shape, lattice, draws, thresholds):
@@ -316,8 +346,8 @@
             vmem((packs, ext, wide), jnp.int32),
             vmem((SWEEPS, LEVELS, 2, ext, LANES), jnp.int32),
             vmem((2, ext, LANES), jnp.int32),
-            vmem((2, DEPTH, wide), jnp.int32),
-            vmem((2, DEPTH, wide), jnp.int32),
+            vmem((2, (DEPTH - 1) * WORD + DEPTH, LANES), jnp.int32),
+            vmem((2, (DEPTH - 1) * WORD + DEPTH, LANES), jnp.int32),
             vmem((rows, LANES), jnp.int32),
             vmem((n_cols - 1, rows, LANES), jnp.int32),
             pltpu.SemaphoreType.DMA((1 + packs,)),
@@ -335,11 +365,11 @@
         unpack_kernel,
         out_shape=(
             jax.ShapeDtypeStruct((rows, cols), jnp.int32),
-            jax.ShapeDtypeStruct((1, LANES), jnp.float32),
+            jax.ShapeDtypeStruct((rows,), jnp.float32),
         ),
         name="unpack",
     )(word, mean)
-    return final, means[0, :rows]
+    return final, means
 
 
 def solution(mesh):

time: 41.3 us -> 37.2 us (0.901)
  Pallas kernels: 39.3 us -> 36.3 us
  local copies, waits for them, and re-layouts: 1.17 us -> 0 us
    pallas_call x1, Pallas kernels: 37.7 us -> 34.7 us  [on_device(): pl.pallas_call(functools.partial(sweep_kernel, shape), out_shape=(jax.Sha...]
    unnamed x2 -> x0, local copies, waits for them, and re-layouts: 0.66 us -> none
    squeeze x1 -> x0, local copies, waits for them, and re-layouts: 0.51 us -> none  [on_device(): return (final, means[0, :rows])]
where the time goes in v1:
time: 37.2 us; the launch traced here: 36.9 us
  Pallas kernels  36.3 us (98%)
  between operations  0.64 us (2%)
    pallas_call x1, Pallas kernels, on_device(): pl.pallas_call(functools.partial(sweep_kernel, shape), out_shape=(jax.Sha...  34.7 us
    pallas_call x1, Pallas kernels, on_device(): pl.pallas_call(unpack_kernel, out_shape=(jax.ShapeDtypeStruct((rows, cols...  1.58 us

profile of v1, /device:TPU:0, one launch (start us, length us, event | category | flops | bytes accessed | tf_op | source)
XLA Modules:
  0.0 36.9 jit_solution(18204324994530244553)
XLA Ops:
  0.6 34.7 %sweeps.1 = (s32[32,128]{1,0:T(8,128)}, f32[1,128]{1,0:T(1,128)}) custom-call(s32[32,4096]{1,0:T(8,128)} %lat_ref.1, s32[2,32,4096]{2,1,0:T(8,128)} %draws_ref.1, s32[5]{0:T(128)} %thr_ref.1), custom_call_target="tpu_custom_call" | custom-call | tf_op jit(solution)/shard_map/sweeps/pallas_call | solution.py:332
  35.4 1.6 %unpack.1 = (s32[32,4096]{1,0:T(8,128)}, f32[32]{0:T(128)}) custom-call(s32[32,128]{1,0:T(8,128)} %get-tuple-element.4.word_ref, f32[1,128]{1,0:T(1,128)} %get-tuple-element.5.row_ref), custom_call_target="tpu_custom_call" | custom-call | tf_op jit(solution)/shard_map/unpack/pallas_call | solution.py:364

commit v2 on v1

--- a/solution.py
+++ b/solution.py
@@ -11,7 +11,8 @@
 LEVELS = 5
 PER_WORD = 4
 BITS = 8
-DEPTH = 8
+DEPTHS = (4, 4, 4, 4)
+HALO = 8
 LANES = 128
 WORD = 32
 MESH = pl.DeviceIdType.MESH
@@ -79,38 +80,42 @@
     rows, cols = lat_ref.shape
     tiles = cols // LANES
     packs = draws_ref.shape[0]
-    ext = rows + 2 * DEPTH
+    ext = rows + 2 * HALO
     r, c = lax.axis_index("rows"), lax.axis_index("cols")
     up, down = lax.rem(r + n_rows - 1, n_rows), lax.rem(r + 1, n_rows)
     left, right = lax.rem(c + n_cols - 1, n_cols), lax.rem(c + 1, n_cols)
 
-    local = [pltpu.make_async_copy(lat_ref, spins.at[pl.ds(DEPTH, rows), pl.ds(0, cols)], local_sem.at[0])]
+    local = [pltpu.make_async_copy(lat_ref, spins.at[pl.ds(HALO, rows), pl.ds(0, cols)], local_sem.at[0])]
     for pack in range(packs):
         local.append(pltpu.make_async_copy(
-            draws_ref.at[pack], draws.at[pack, pl.ds(DEPTH, rows), pl.ds(0, cols)], local_sem.at[1 + pack]))
+            draws_ref.at[pack], draws.at[pack, pl.ds(HALO, rows), pl.ds(0, cols)], local_sem.at[1 + pack]))
     for copy in local:
         copy.start()
 
     barrier = pltpu.get_barrier_semaphore()
-    around = [(a, b) for a in (up, r, down) for b in (left, c, right)]
-    del around[4]
+    around = [(up, c), (down, c), (r, left), (r, right)]
     others = [lax.rem(c + k, n_cols) for k in range(1, n_cols)]
     for target in around + [(r, b) for b in others[1:-1]]:
         pl.semaphore_signal(barrier, inc=1, device_id=target, device_id_type=MESH)
     pl.semaphore_wait(barrier, len(around) + n_cols - 3)
 
     def row_part(depth):
-        return {-1: (0, depth, DEPTH + rows), 0: (0, rows, DEPTH), 1: (rows - depth, depth, DEPTH - depth)}
+        return {-1: (0, depth, HALO + rows), 0: (0, rows, HALO), 1: (rows - depth, depth, HALO - depth)}
 
     col_part = {-1: (0, LANES, cols + LANES), 0: (0, cols, 0), 1: (cols - LANES, LANES, cols)}
     row_id = {-1: up, 0: r, 1: down}
     col_id = {-1: left, 0: c, 1: right}
-    sides = [(0, -1), (0, 1), (-1, -1), (-1, 1), (1, -1), (1, 1), (-1, 0), (1, 0)]
-    strips, first, later = [], [], []
+    sides = [(-1, 0), (1, 0), (0, -1), (0, 1)]
+    done = [sum(DEPTHS[:turn + 1]) for turn in range(len(DEPTHS))]
+    word_span = 2 * PER_WORD
+    reach = [DEPTHS[0]] + [
+        max(d for d, end in zip(DEPTHS, done) if end - d < word_span * (p + 1) and end > word_span * p) - 1
+        for p in range(packs)
+    ]
 
     def send(stage, index):
         dr, dc = sides[index]
-        r0, rn, rd = row_part(DEPTH - min(stage, 1))[dr]
+        r0, rn, rd = row_part(reach[stage])[dr]
         c0, cn, cd = col_part[dc]
         src, dst = (lat_ref, spins) if stage == 0 else (draws_ref.at[stage - 1], draws.at[stage - 1])
         copy = pltpu.make_async_remote_copy(
@@ -124,14 +129,22 @@
         copy.start()
         return copy
 
-    for stage in range(1 + packs):
-        strips += [send(stage, index) for index in (0, 1)]
-    for stage in range(1 + packs):
-        copies = [send(stage, index) for index in range(2, len(sides))]
-        if stage <= 1:
-            first += copies
-        else:
-            later += copies
+    def pass_on(stage, index):
+        r0, rn, rd = row_part(reach[stage])[sides[index][0]]
+        block = spins if stage == 0 else draws.at[stage - 1]
+        copy = pltpu.make_async_remote_copy(
+            src_ref=block.at[pl.ds(HALO + r0, rn), pl.ds(cols, 2 * LANES)],
+            dst_ref=block.at[pl.ds(rd, rn), pl.ds(cols, 2 * LANES)],
+            send_sem=send_sem.at[stage, 4 + index],
+            recv_sem=recv_sem.at[stage, 4 + index],
+            device_id=(row_id[sides[index][0]], c),
+            device_id_type=MESH,
+        )
+        copy.start()
+        return copy
+
+    first = [send(stage, index) for stage in (0, 1) for index in (0, 1)]
+    strips = [send(stage, index) for stage in range(1 + packs) for index in (2, 3)]
 
     bit_masks = []
     for level in range(LEVELS):
@@ -175,7 +188,7 @@
             tile_of(spins, row0, tiles + 1) & 2)
 
     groups = rows // 8
-    halo = DEPTH // 8
+    halo = HALO // 8
 
     for copy in local:
         copy.wait()
@@ -184,13 +197,14 @@
     def _(group):
         pack_group(group)
 
+    for copy in strips:
+        copy.wait()
+    first += [pass_on(stage, index) for stage in (0, 1) for index in (0, 1)]
+
     @pl.loop(0, packs * groups)
     def _(step):
         prepare(step // groups, halo + step % groups)
 
-    for copy in strips:
-        copy.wait()
-
     @pl.loop(halo, halo + groups)
     def _(group):
         pack_side(group)
@@ -201,6 +215,7 @@
 
     for copy in first:
         copy.wait()
+    later = [step(stage, index) for stage in range(2, 1 + packs) for index in (0, 1) for step in (send, pass_on)]
 
     for group in (0, halo + groups):
         pack_group(group)
@@ -212,7 +227,7 @@
         prepare_side(0, side * (halo + groups))
 
     lane = lax.broadcasted_iota(jnp.int32, (ext, LANES), 1)
-    base = r * rows + c * cols - DEPTH
+    base = r * rows + c * cols - HALO
     site = lax.broadcasted_iota(jnp.int32, (ext, LANES), 0) + lane + base
     odd_sites = -(site & 1)
 
@@ -227,69 +242,81 @@
         state[0] = main
         state[1] = side
 
-    half = DEPTH // 2
-
-    @pl.loop(0, half)
-    def _(t):
-        sweep(t)
-
-    copies = []
     tile_id = lax.broadcasted_iota(jnp.int32, (WORD, LANES), 0)
-    sub, lane8 = (lax.broadcasted_iota(jnp.int32, (DEPTH, LANES), d) for d in (0, 1))
+    sub, lane8 = (lax.broadcasted_iota(jnp.int32, (HALO, LANES), d) for d in (0, 1))
     low_lanes = lane8 < LANES // 2
-    near, far = (0, DEPTH - 1), (DEPTH - 1, 0)
-    for index, (row0, dev) in enumerate(((DEPTH, up), (rows, down))):
-        main, side = state[0, pl.ds(row0, DEPTH), :], state[1, pl.ds(row0, DEPTH), :]
-        odd = odd_sites[row0:row0 + DEPTH]
-        joint = (main & odd) | (pltpu.roll(main, 1 if index == 0 else DEPTH - 1, 0) & ~odd)
-        main = jnp.where(sub == near[index], joint, main)
-        for i in range(DEPTH - 1):
-            row = main[i + index:i + index + 1]
-            out_edge[index, pl.ds(i * WORD, WORD), :] = shr(jnp.broadcast_to(row, (WORD, LANES)), tile_id) & 1
-        out_edge[index, pl.ds((DEPTH - 1) * WORD, DEPTH), :] = jnp.where(low_lanes, shr(side, jnp.int32(1)), side) & 1
-        copy = pltpu.make_async_remote_copy(
-            src_ref=out_edge.at[index],
-            dst_ref=in_edge.at[index],
-            send_sem=edge_send.at[index],
-            recv_sem=edge_recv.at[index],
-            device_id=(dev, c),
-            device_id_type=MESH,
-        )
-        copy.start()
-        copies.append(copy)
-
-    for copy in later:
-        copy.wait()
-
-    @pl.loop(0, 2)
-    def _(side):
-        prepare(1, side * (halo + groups))
-        prepare_side(1, side * (halo + groups))
-
-    for index, (row0, copy) in enumerate(((DEPTH + rows, copies[0]), (0, copies[1]))):
-        copy.wait()
-        old = state[0, pl.ds(row0, DEPTH), :]
-        odd = odd_sites[row0:row0 + DEPTH]
-        word = old
-        for i in range(DEPTH - 1):
-            bits = in_edge[index, pl.ds(i * WORD, WORD), :] << tile_id
-            row = bits[0:8] | bits[8:16] | bits[16:24] | bits[24:32]
-            for shift in (4, 2, 1):
-                row = row | pltpu.roll(row, shift, 0)
-            at = i + index
-            if at == near[index]:
-                word = jnp.where(sub == far[index], row, word)
-                row = (old & ~odd) | (row & odd)
-            word = jnp.where(sub == at, row, word)
-        state[0, pl.ds(row0, DEPTH), :] = word
-        bits = in_edge[index, pl.ds((DEPTH - 1) * WORD, DEPTH), :]
-        state[1, pl.ds(row0, DEPTH), :] = jnp.where(low_lanes, bits << 1, bits)
-
-    @pl.loop(half, SWEEPS)
-    def _(t):
-        sweep(t)
-
-    final = state[0, pl.ds(DEPTH, rows), :]
+    near = (0, HALO - 1)
+    side_rows = pl.ds(0, HALO)
+
+    def places(depth):
+        return (depth - 1, HALO - depth), (0, HALO - depth + 1), pl.ds(0, HALO + (depth - 1) * WORD)
+
+    def send_edges(turn, depth):
+        copies = []
+        far, start, whole = places(depth)
+        for index, (row0, dev) in enumerate(((HALO, up), (rows, down))):
+            main, side = state[0, pl.ds(row0, HALO), :], state[1, pl.ds(row0, HALO), :]
+            odd = odd_sites[row0:row0 + HALO]
+            shift = (near[index] - far[index]) % HALO
+            main = jnp.where(sub == near[index], (main & odd) | (pltpu.roll(main, shift, 0) & ~odd), main)
+            for i in range(depth - 1):
+                row = main[i + start[index]:i + start[index] + 1]
+                bits = shr(jnp.broadcast_to(row, (WORD, LANES)), tile_id) & 1
+                out_edge[turn, index, pl.ds(HALO + i * WORD, WORD), :] = bits
+            out_edge[turn, index, side_rows, :] = jnp.where(low_lanes, shr(side, jnp.int32(1)), side) & 1
+            copy = pltpu.make_async_remote_copy(
+                src_ref=out_edge.at[turn, index, whole],
+                dst_ref=in_edge.at[turn, index, whole],
+                send_sem=edge_send.at[turn, index],
+                recv_sem=edge_recv.at[turn, index],
+                device_id=(dev, c),
+                device_id_type=MESH,
+            )
+            copy.start()
+            copies.append(copy)
+        return copies
+
+    def take_edges(turn, depth, copies):
+        far, start, _ = places(depth)
+        for index, (row0, copy) in enumerate(((HALO + rows, copies[0]), (0, copies[1]))):
+            copy.wait()
+            old = state[0, pl.ds(row0, HALO), :]
+            odd = odd_sites[row0:row0 + HALO]
+            word = old
+            for i in range(depth - 1):
+                bits = in_edge[turn, index, pl.ds(HALO + i * WORD, WORD), :] << tile_id
+                row = bits[0:8] | bits[8:16] | bits[16:24] | bits[24:32]
+                for shift in (4, 2, 1):
+                    row = row | pltpu.roll(row, shift, 0)
+                at = i + start[index]
+                if at == near[index]:
+                    word = jnp.where(sub == far[index], row, word)
+                    row = (old & ~odd) | (row & odd)
+                word = jnp.where(sub == at, row, word)
+            state[0, pl.ds(row0, HALO), :] = word
+            bits = in_edge[turn, index, side_rows, :]
+            state[1, pl.ds(row0, HALO), :] = jnp.where(low_lanes, bits << 1, bits)
+
+    for turn, depth in enumerate(DEPTHS):
+
+        @pl.loop((done[turn] - depth) // 2, done[turn] // 2)
+        def _(t):
+            sweep(t)
+
+        if turn + 1 < len(DEPTHS):
+            copies = send_edges(turn, DEPTHS[turn + 1])
+            if done[turn] == word_span:
+                for copy in later:
+                    copy.wait()
+
+                @pl.loop(0, 2)
+                def _(side):
+                    prepare(1, side * (halo + groups))
+                    prepare_side(1, side * (halo + groups))
+
+            take_edges(turn, DEPTHS[turn + 1], copies)
+
+    final = state[0, pl.ds(HALO, rows), :]
     word_ref[...] = final
     count[...] = lax.population_count(final)
     copies = []
@@ -325,9 +352,10 @@
 def on_device(shape, lattice, draws, thresholds):
     rows, cols = lattice.shape
     packs = draws.shape[0]
-    assert cols == WORD * LANES and rows <= LANES and rows % 8 == 0 and 2 * DEPTH == 2 * SWEEPS
-    ext, wide = rows + 2 * DEPTH, cols + 2 * LANES
+    assert cols == WORD * LANES and rows <= LANES and rows % 8 == 0 and sum(DEPTHS) == 2 * SWEEPS
+    ext, wide = rows + 2 * HALO, cols + 2 * LANES
     n_cols = shape[1]
+    turns = len(DEPTHS) - 1
     vmem, hbm = pltpu.VMEM, pl.ANY
     word, mean = pl.pallas_call(
         functools.partial(sweep_kernel, shape),
@@ -346,15 +374,15 @@
             vmem((packs, ext, wide), jnp.int32),
             vmem((SWEEPS, LEVELS, 2, ext, LANES), jnp.int32),
             vmem((2, ext, LANES), jnp.int32),
-            vmem((2, (DEPTH - 1) * WORD + DEPTH, LANES), jnp.int32),
-            vmem((2, (DEPTH - 1) * WORD + DEPTH, LANES), jnp.int32),
+            vmem((turns, 2, (max(DEPTHS) - 1) * WORD + HALO, LANES), jnp.int32),
+            vmem((turns, 2, (max(DEPTHS) - 1) * WORD + HALO, LANES), jnp.int32),
             vmem((rows, LANES), jnp.int32),
             vmem((n_cols - 1, rows, LANES), jnp.int32),
             pltpu.SemaphoreType.DMA((1 + packs,)),
             pltpu.SemaphoreType.DMA((1 + packs, 8)),
             pltpu.SemaphoreType.DMA((1 + packs, 8)),
-            pltpu.SemaphoreType.DMA((2,)),
-            pltpu.SemaphoreType.DMA((2,)),
+            pltpu.SemaphoreType.DMA((turns, 2)),
+            pltpu.SemaphoreType.DMA((turns, 2)),
             pltpu.SemaphoreType.DMA((n_cols - 1,)),
             pltpu.SemaphoreType.DMA((n_cols - 1,)),
         ],

time: 37.2 us -> 36.1 us (0.970)
  Pallas kernels: 36.3 us -> 35.2 us
    pallas_call x1, Pallas kernels: 34.7 us -> 33.6 us  [on_device(): pl.pallas_call(functools.partial(sweep_kernel, shape), out_shape=(jax.Sha...]
where the time goes in v2:
time: 36.1 us; the launch traced here: 35.8 us
  Pallas kernels  35.2 us (98%)
  between operations  0.64 us (2%)
    pallas_call x1, Pallas kernels, on_device(): pl.pallas_call(functools.partial(sweep_kernel, shape), out_shape=(jax.Sha...  33.6 us
    pallas_call x1, Pallas kernels, on_device(): pl.pallas_call(unpack_kernel, out_shape=(jax.ShapeDtypeStruct((rows, cols...  1.58 us

profile of v2, /device:TPU:0, one launch (start us, length us, event | category | flops | bytes accessed | tf_op | source)
XLA Modules:
  0.0 35.8 jit_solution(10767903044062256638)
XLA Ops:
  0.6 33.6 %sweeps.1 = (s32[32,128]{1,0:T(8,128)}, f32[1,128]{1,0:T(1,128)}) custom-call(s32[32,4096]{1,0:T(8,128)} %lat_ref.1, s32[2,32,4096]{2,1,0:T(8,128)} %draws_ref.1, s32[5]{0:T(128)} %thr_ref.1), custom_call_target="tpu_custom_call" | custom-call | tf_op jit(solution)/shard_map/sweeps/pallas_call | solution.py:360
  34.2 1.6 %unpack.1 = (s32[32,4096]{1,0:T(8,128)}, f32[32]{0:T(128)}) custom-call(s32[32,128]{1,0:T(8,128)} %get-tuple-element.4.word_ref, f32[1,128]{1,0:T(1,128)} %get-tuple-element.5.row_ref), custom_call_target="tpu_custom_call" | custom-call | tf_op jit(solution)/shard_map/unpack/pallas_call | solution.py:392

commit v3 on v2

--- a/solution.py
+++ b/solution.py
@@ -11,7 +11,7 @@
 LEVELS = 5
 PER_WORD = 4
 BITS = 8
-DEPTHS = (4, 4, 4, 4)
+DEPTHS = (4, 4, 8)
 HALO = 8
 LANES = 128
 WORD = 32
@@ -200,6 +200,7 @@
     for copy in strips:
         copy.wait()
     first += [pass_on(stage, index) for stage in (0, 1) for index in (0, 1)]
+    later = [step(stage, index) for stage in range(2, 1 + packs) for index in (0, 1) for step in (send, pass_on)]
 
     @pl.loop(0, packs * groups)
     def _(step):
@@ -215,7 +216,6 @@
 
     for copy in first:
         copy.wait()
-    later = [step(stage, index) for stage in range(2, 1 + packs) for index in (0, 1) for step in (send, pass_on)]
 
     for group in (0, halo + groups):
         pack_group(group)

time: 36.1 us -> 34.3 us (0.950)
  Pallas kernels: 35.2 us -> 33.4 us
    pallas_call x1, Pallas kernels: 33.6 us -> 31.8 us  [on_device(): pl.pallas_call(functools.partial(sweep_kernel, shape), out_shape=(jax.Sha...]
where the time goes in v3:
time: 34.3 us; the launch traced here: 34 us
  Pallas kernels  33.4 us (97%)
  between operations  0.64 us (2%)
    pallas_call x1, Pallas kernels, on_device(): pl.pallas_call(functools.partial(sweep_kernel, shape), out_shape=(jax.Sha...  31.8 us
    pallas_call x1, Pallas kernels, on_device(): pl.pallas_call(unpack_kernel, out_shape=(jax.ShapeDtypeStruct((rows, cols...  1.58 us

profile of v3, /device:TPU:0, one launch (start us, length us, event | category | flops | bytes accessed | tf_op | source)
XLA Modules:
  0.0 34.0 jit_solution(1356017160731091984)
XLA Ops:
  0.6 31.8 %sweeps.1 = (s32[32,128]{1,0:T(8,128)}, f32[1,128]{1,0:T(1,128)}) custom-call(s32[32,4096]{1,0:T(8,128)} %lat_ref.1, s32[2,32,4096]{2,1,0:T(8,128)} %draws_ref.1, s32[5]{0:T(128)} %thr_ref.1), custom_call_target="tpu_custom_call" | custom-call | tf_op jit(solution)/shard_map/sweeps/pallas_call | solution.py:360
  32.5 1.6 %unpack.1 = (s32[32,4096]{1,0:T(8,128)}, f32[32]{0:T(128)}) custom-call(s32[32,128]{1,0:T(8,128)} %get-tuple-element.4.word_ref, f32[1,128]{1,0:T(1,128)} %get-tuple-element.5.row_ref), custom_call_target="tpu_custom_call" | custom-call | tf_op jit(solution)/shard_map/unpack/pallas_call | solution.py:392
